TPU v7x, 32 devices: a whole 2x2x4 slice. The times are simulated.
32 devices in a mesh: blk: 16 (over z, y, core), uly: 2 (over x).
Axes of the slice: x: 2, y: 2, z: 4, core: 2. Of those that a mesh axis runs over, the one named last changes fastest.
Arguments:
- footage_probes: bfloat16 [1024, 32, 64], P(('blk', 'uly')), may hold values from -6 to 6
- footage_lookup_keys: bfloat16 [1024, 32, 64], P(('blk', 'uly')), may hold values from -6 to 6
- footage_payload: bfloat16 [1024, 32, 64], P(('blk', 'uly')), may hold values from -6 to 6
- caption_probes: bfloat16 [256, 32, 64], replicated, may hold values from -6 to 6
- caption_lookup_keys: bfloat16 [256, 32, 64], replicated, may hold values from -6 to 6
- caption_payload: bfloat16 [256, 32, 64], replicated, may hold values from -6 to 6
- footage_probes_amplitude: float32 [64], replicated, may hold values from 0.25 to 1.75
- footage_keys_amplitude: float32 [64], replicated, may hold values from 0.25 to 1.75
- caption_probes_amplitude: float32 [64], replicated, may hold values from 0.25 to 1.75
- caption_keys_amplitude: float32 [64], replicated, may hold values from 0.25 to 1.75
- focus_sharpness: float32 [32], replicated, may hold values from 1.5 to 4
- caption_validity: int32 [256], replicated, may hold values 0 or 1
Outputs:
- vid_out: bfloat16 [1024, 32, 64], P(('blk', 'uly'))
- txt_out: bfloat16 [256, 32, 64], P('uly', 'blk')
Inputs may be any that keep to these rules, and one draw needn't show every extreme that they name: caption_validity holds only 0 and 1.
All inputs are finite; a program needn't handle non-finite values.
Results may differ from a plain program's by a relative error of at most 0.0035.
Values may be sent and summed in bfloat16 or wider, within the bound.
A program may use at most 64 MiB of HBM per device.

v0:
```python
import math

import jax
import jax.numpy as jnp
from jax import lax
from jax.sharding import PartitionSpec as P

EPSILON = 1e-06
NEGATIVE = -1e30


def normed(tensor, gain_vector, rescale_factor):
    widened = tensor.astype(jnp.float32)
    inverse = lax.rsqrt(jnp.mean(widened * widened, axis=-1, keepdims=True) + EPSILON)
    return (widened * inverse * gain_vector * rescale_factor).astype(jnp.bfloat16)


def fragment_contributions(queries, key_rows, value_rows, valid):
    scores = jnp.einsum("qhd,khd->hqk", queries, key_rows, preferred_element_type=jnp.float32)
    if valid is not None:
        scores = jnp.where(valid[None, None, :], scores, NEGATIVE)
    maxima = jnp.max(scores, axis=-1)
    weights = jnp.exp(scores - maxima[..., None])
    if valid is not None:
        weights = jnp.where(valid[None, None, :], weights, 0.0)
    totals = jnp.sum(weights, axis=-1)
    accum = jnp.einsum(
        "hqk,khd->hqd", weights, value_rows.astype(jnp.float32), precision=lax.Precision.HIGHEST
    )
    return (maxima, totals, accum)


def combine(earlier, later):
    max_one, total_one, accum_one = earlier
    max_two, total_two, accum_two = later
    merged_max = jnp.maximum(max_one, max_two)
    factor_one = jnp.exp(max_one - merged_max)
    factor_two = jnp.exp(max_two - merged_max)
    merged_total = total_one * factor_one + total_two * factor_two
    merged_accum = accum_one * factor_one[..., None] + accum_two * factor_two[..., None]
    return (merged_max, merged_total, merged_accum)


def on_device(
    footage_probes,
    footage_lookup_keys,
    footage_payload,
    caption_probes,
    caption_lookup_keys,
    caption_payload,
    footage_probes_amplitude,
    footage_keys_amplitude,
    caption_probes_amplitude,
    caption_keys_amplitude,
    focus_sharpness,
    caption_validity,
):
    channel_width = footage_probes.shape[2]
    rescale_factor = focus_sharpness[None, :, None] / math.sqrt(channel_width)
    q_norm = normed(footage_probes, footage_probes_amplitude, rescale_factor)
    k_norm = normed(footage_lookup_keys, footage_keys_amplitude, 1.0)
    q_local = lax.all_to_all(q_norm, "blk", split_axis=1, concat_axis=0, tiled=True)
    k_local = lax.all_to_all(k_norm, "blk", split_axis=1, concat_axis=0, tiled=True)
    v_local = lax.all_to_all(footage_payload, "blk", split_axis=1, concat_axis=0, tiled=True)
    local_heads = q_local.shape[1]
    head_start = lax.axis_index("blk") * local_heads
    local_scale = lax.dynamic_slice_in_dim(rescale_factor, head_start, local_heads, 1)
    text_q = normed(
        lax.dynamic_slice_in_dim(caption_probes, head_start, local_heads, 1),
        caption_probes_amplitude,
        local_scale,
    )
    text_k = normed(
        lax.dynamic_slice_in_dim(caption_lookup_keys, head_start, local_heads, 1),
        caption_keys_amplitude,
        1.0,
    )
    text_v = lax.dynamic_slice_in_dim(caption_payload, head_start, local_heads, 1)
    text_valid = caption_validity == 1
    text_share = caption_probes.shape[0] // lax.axis_size("uly")
    row_start = lax.axis_index("uly") * text_share
    video_rows = q_local.shape[0]
    queries = jnp.concatenate(
        [q_local, lax.dynamic_slice_in_dim(text_q, row_start, text_share, 0)], 0
    )

    def fold_inward(running, gathered):
        key_block, value_block = gathered
        row_count = key_block.shape[0]
        block_rows = math.gcd(row_count, 512)

        def absorb_block(block_index, running_state):
            key_part = lax.dynamic_slice_in_dim(key_block, block_index * block_rows, block_rows, 0)
            value_part = lax.dynamic_slice_in_dim(
                value_block, block_index * block_rows, block_rows, 0
            )
            return combine(
                running_state, fragment_contributions(queries, key_part, value_part, None)
            )

        return lax.fori_loop(0, row_count // block_rows, absorb_block, running)

    first_state = fragment_contributions(queries, text_k, text_v, text_valid)
    maxima, totals, accum = fold_inward(
        first_state,
        (
            lax.all_gather(k_local, "uly", axis=0, tiled=True),
            lax.all_gather(v_local, "uly", axis=0, tiled=True),
        ),
    )
    attended = jnp.transpose(accum / totals[..., None], (1, 0, 2)).astype(jnp.bfloat16)
    vid_out = lax.all_to_all(attended[:video_rows], "blk", split_axis=0, concat_axis=1, tiled=True)
    txt_out = attended[video_rows:]
    return (vid_out, txt_out)


def solution(mesh):
    return jax.shard_map(
        on_device,
        mesh=mesh,
        in_specs=(
            P(("blk", "uly"), None, None),
            P(("blk", "uly"), None, None),
            P(("blk", "uly"), None, None),
            P(),
            P(),
            P(),
            P(),
            P(),
            P(),
            P(),
            P(),
            P(),
        ),
        out_specs=(P(("blk", "uly"), None, None), P("uly", "blk", None)),
        check_vma=False,
    )
```

profile of v0, /device:TPU:0, one launch (start us, length us, event | category | flops | bytes accessed | tf_op | source)
XLA Modules:
  0.0 76.9 jit_solution(12764766947317799488)
XLA Ops:
  0.7 0.8 broadcast_multiply_fusion
  1.4 1.2 %fusion.21 = f32[32,32]{0,1:T(8,128)S(1)} fusion(bf16[32,32,64]{2,1,0:T(8,128)(2,1)} %param.14), kind=kLoop, calls=%fused_computation.27 | loop fusion | flops 195584 | bytes 135168 | tf_op jit(solution)/shard_map/reduce_sum | solution.py:14
  2.6 1.2 %fusion.44 = bf16[32,32,64]{2,1,0:T(8,128)(2,1)S(1)} fusion(f32[32]{0:T(128)S(1)} %broadcast_multiply_fusion, f32[64]{0:T(128)} %param.20, f32[32,32]{0,1:T(8,128)S(1)} %add_rsqrt_fusion.1, bf16[32,32,64]{2,1,0:T(8,128)(2,1)} %param.14), kind=kLoop, calls=%fused_computation.64 | loop fusion | flops 327680 | bytes 266624
  3.8 0.9 %reshape.50 = bf16[16,2,2048]{2,1,0:T(2,128)(2,1)} reshape(bf16[32,32,64]{2,1,0:T(8,128)(2,1)S(1)} %fusion.44) | data formatting | bytes 262144
  4.7 7.4 %all-to-all-start = ((bf16[16,2,2048]{2,1,0:T(2,128)(2,1)}), bf16[16,2,2048]{2,1,0:T(2,128)(2,1)S(1)}, u32[]{:S(2)}, u32[]{:S(2)}) async-start(bf16[16,2,2048]{2,1,0:T(2,128)(2,1)} %reshape.50), calls=%async_computation | async-start | bytes 262144 | tf_op jit(solution)/shard_map/all_to_all | solution.py:62
  12.2 0.9 %fusion.28 = (f32[256,2]{0,1:T(2,128)S(1)}, f32[256,2]{0,1:T(2,128)S(1)}) fusion(bf16[256,32,64]{0,2,1:T(8,128)(2,1)} %param.18, s32[]{:T(128)S(6)} %select_n.24, bf16[256,32,64]{0,2,1:T(8,128)(2,1)} %param.17), kind=kLoop, calls=%fused_computation.38 | loop fusion | flops 195584 | bytes 135172 | tf_op jit(solution)/shard_map/reduce_sum | solution.py:14
  13.6 0.9 %dynamic-slice_convert_fusion = f32[256,2,64]{0,2,1:T(8,128)S(1)} fusion(bf16[256,32,64]{0,2,1:T(8,128)(2,1)} %param.17, s32[]{:T(128)S(6)} %select_n.24), kind=kLoop, calls=%fused_computation.49 | loop fusion | flops 32768 | bytes 196612 | tf_op jit(solution)/shard_map/convert_element_type | solution.py:13
  14.5 0.9 %reshape.52 = bf16[16,2,2048]{2,1,0:T(2,128)(2,1)} reshape(bf16[32,32,64]{2,1,0:T(8,128)(2,1)S(1)} %fusion.43) | data formatting | bytes 262144
  15.4 4.7 %all-to-all-done = bf16[16,2,2048]{2,1,0:T(2,128)(2,1)S(1)} async-done(((bf16[16,2,2048]{2,1,0:T(2,128)(2,1)}), bf16[16,2,2048]{2,1,0:T(2,128)(2,1)S(1)}, u32[]{:S(2)}, u32[]{:S(2)}) %all-to-all-start) | async-done | bytes 131104 | tf_op jit(solution)/shard_map/all_to_all | solution.py:62
  20.1 3.5 %all-to-all-start.1 = ((bf16[16,2,2048]{2,1,0:T(2,128)(2,1)}), bf16[16,2,2048]{2,1,0:T(2,128)(2,1)S(1)}, u32[]{:S(2)}, u32[]{:S(2)}) async-start(bf16[16,2,2048]{2,1,0:T(2,128)(2,1)} %reshape.52), calls=%async_computation.1 | async-start | bytes 262144 | tf_op jit(solution)/shard_map/all_to_all | solution.py:63
  23.8 0.9 %reshape.54 = bf16[16,2,2048]{2,1,0:T(2,128)(2,1)} reshape(bf16[32,32,64]{2,1,0:T(8,128)(2,1)S(1)} %bitcast.58) | data formatting | bytes 262144
  24.8 6.7 %all-to-all-done.1 = bf16[16,2,2048]{2,1,0:T(2,128)(2,1)S(1)} async-done(((bf16[16,2,2048]{2,1,0:T(2,128)(2,1)}), bf16[16,2,2048]{2,1,0:T(2,128)(2,1)S(1)}, u32[]{:S(2)}, u32[]{:S(2)}) %all-to-all-start.1) | async-done | bytes 131104 | tf_op jit(solution)/shard_map/all_to_all | solution.py:63
  31.5 3.5 %all-to-all-start.2 = ((bf16[16,2,2048]{2,1,0:T(2,128)(2,1)}), bf16[16,2,2048]{2,1,0:T(2,128)(2,1)S(1)}, u32[]{:S(2)}, u32[]{:S(2)}) async-start(bf16[16,2,2048]{2,1,0:T(2,128)(2,1)} %reshape.54), calls=%async_computation.2 | async-start | bytes 262144 | tf_op jit(solution)/shard_map/all_to_all | solution.py:64
  35.6 9.2 %all_gather.6 = bf16[1024,2,64]{2,0,1:T(8,128)(2,1)S(1)} all-gather(bf16[512,2,64]{2,0,1:T(8,128)(2,1)S(1)} %bitcast.50), channel_id=1, replica_groups=mesh['blk'=16,'uly'=2] {'uly'}, dimensions={0}, use_global_device_ids=true | all-gather | bytes 393216 | tf_op jit(solution)/shard_map/all_gather | solution.py:107
  45.3 8.3 %all_gather.7 = bf16[1024,2,64]{2,0,1:T(8,128)(2,1)S(1)} all-gather(bf16[512,2,64]{2,0,1:T(8,128)(2,1)S(1)} %bitcast.51), channel_id=1, replica_groups=mesh['blk'=16,'uly'=2] {'uly'}, dimensions={0}, use_global_device_ids=true | all-gather | bytes 393216 | tf_op jit(solution)/shard_map/all_gather | solution.py:108
  53.8 1.3 %fusion.42 = (f32[2,640]{1,0:T(2,128)S(1)}, f32[2,640,256]{1,2,0:T(8,128)S(1)}) fusion(f32[64]{0:T(128)S(1)} %copy-done.5, f32[256,2]{0,1:T(2,128)S(1)} %add_rsqrt_fusion.2, bf16[256,32,64]{0,2,1:T(8,128)(2,1)} %param.18, s32[]{:T(128)S(6)} %select_n.24, bf16[128,2,64]{0,2,1:T(8,128)(2,1)S(1)} %fusion.34, bf16[512,2,64]{0,2,1:T(8,128)(2,1)S(1)} %copy.45, ...), kind=kOutput, calls=%fused_computation.61 | convolution fusion | flops 43055872 | bytes 1547780 | tf_op jit(solution)/shard_map/qhd,khd->hqk/dot_general | solution.py:19
  55.4 0.8 %fusion.16 = f32[2,640,64]{1,2,0:T(8,128)S(1)} fusion(f32[2,640,256]{1,2,0:T(8,128)S(1)} %get-tuple-element.177, f32[2,640]{1,0:T(2,128)S(1)} %get-tuple-element.236, pred[256]{0:T(512)(128)(4,1)S(1)} %broadcast_compare_fusion, bf16[256,32,64]{0,2,1:T(8,128)(2,1)S(1)} %copy-done, s32[]{:T(128)S(6)} %select_n.24), kind=kOutput, calls=%fused_computation.18 | convolution fusion | flops 252313600 | bytes 1709572 | tf_op jit(solution)/shard_map/hqk,khd->hqd/dot_general | solution.py:27
  56.2 4.7 %while.17 = (s32[]{:T(128)}, f32[2,640]{1,0:T(2,128)S(1)}, f32[2,640]{1,0:T(2,128)S(1)}, f32[2,640,64]{1,2,0:T(8,128)S(1)}, bf16[1024,2,64]{0,2,1:T(8,128)(2,1)S...) while((s32[]{:T(128)}, f32[2,640]{1,0:T(2,128)S(1)}, ...), condition=%wide.region_9.10_spmd, body=%wide.region_6.9_spmd.sunk | while | flops 590074880 | bytes 9017507 | solution.py:101
  57.2 1.4 %fusion.55 = f32[2,640,64]{1,2,0:T(8,128)S(1)} fusion(f32[2,512,640]{2,1,0:T(8,128)S(1)} %get-tuple-element.229, f32[2,640]{1,0:T(2,128)S(1)} %get-tuple-element.230, f32[2,640,64]{1,2,0:T(8,128)S(1)} %get-tuple-element.249, f32[2,640]{1,0:T(2,128)S(1)} %get-tuple-element.233, f32[2,640]{1,0:T(2,128)S(1)} %get-tuple-element.234, ...), kind=kOutput, calls=%fused_computation.7.clone.1 | convolution fusion | flops 504217600 | bytes 3423236 | tf_op jit(solution)/shard_map/while/body/eval_jaxpr/hqk,khd->hqd/dot_general | solution.py:27
  59.5 1.3 %fusion.55 = f32[2,640,64]{1,2,0:T(8,128)S(1)} fusion(f32[2,512,640]{2,1,0:T(8,128)S(1)} %get-tuple-element.229, f32[2,640]{1,0:T(2,128)S(1)} %get-tuple-element.230, f32[2,640,64]{1,2,0:T(8,128)S(1)} %get-tuple-element.249, f32[2,640]{1,0:T(2,128)S(1)} %get-tuple-element.233, f32[2,640]{1,0:T(2,128)S(1)} %get-tuple-element.234, ...), kind=kOutput, calls=%fused_computation.7.clone.1 | convolution fusion | flops 504217600 | bytes 3423236 | tf_op jit(solution)/shard_map/while/body/eval_jaxpr/hqk,khd->hqd/dot_general | solution.py:27
  61.4 0.9 %reshape.56 = bf16[16,2,2048]{2,1,0:T(2,128)(2,1)} reshape(bf16[512,2,64]{2,1,0:T(2,128)(2,1)S(1)} %slice.8) | data formatting | bytes 262144
  62.3 5.6 %all-to-all-start.3 = ((bf16[16,2,2048]{2,1,0:T(2,128)(2,1)}), bf16[16,2,2048]{2,1,0:T(2,128)(2,1)S(1)}, u32[]{:S(2)}, u32[]{:S(2)}) async-start(bf16[16,2,2048]{2,1,0:T(2,128)(2,1)} %reshape.56), calls=%async_computation.3 | async-start | bytes 262144 | tf_op jit(solution)/shard_map/all_to_all | solution.py:112
  68.7 7.1 %all-to-all-done.3 = bf16[16,2,2048]{2,1,0:T(2,128)(2,1)S(1)} async-done(((bf16[16,2,2048]{2,1,0:T(2,128)(2,1)}), bf16[16,2,2048]{2,1,0:T(2,128)(2,1)S(1)}, u32[]{:S(2)}, u32[]{:S(2)}) %all-to-all-start.3) | async-done | bytes 131104 | tf_op jit(solution)/shard_map/all_to_all | solution.py:112
  76.1 0.8 %copy.58 = bf16[32,32,64]{2,1,0:T(8,128)(2,1)} copy(bf16[32,32,64]{2,0,1:T(8,128)(2,1)S(1)} %bitcast.57) | data formatting | bytes 262144
  (51 shorter events, 5.6 us)
Async XLA Ops:
  0.6 54.8 %copy-start = (bf16[256,32,64]{0,2,1:T(8,128)(2,1)S(1)}, bf16[256,32,64]{0,2,1:T(8,128)(2,1)}, u32[]{:S(2)}) copy-start(bf16[256,32,64]{0,2,1:T(8,128)(2,1)} %param.19) | copy-start | bytes 3145732
  0.6 12.5 %copy-start.1 = (bf16[32,32,64]{2,1,0:T(8,128)(2,1)S(1)}, bf16[32,32,64]{2,1,0:T(8,128)(2,1)}, u32[]{:S(2)}) copy-start(bf16[32,32,64]{2,1,0:T(8,128)(2,1)} %param.15) | copy-start | bytes 393220
  0.7 12.7 %copy-start.3 = (f32[64]{0:T(128)S(1)}, f32[64]{0:T(128)}, u32[]{:S(2)}) copy-start(f32[64]{0:T(128)} %param.21) | copy-start | bytes 772
  3.8 19.9 %copy-start.2 = (bf16[32,32,64]{2,1,0:T(8,128)(2,1)S(1)}, bf16[32,32,64]{2,1,0:T(8,128)(2,1)}, u32[]{:S(2)}) copy-start(bf16[32,32,64]{2,1,0:T(8,128)(2,1)} %param.16) | copy-start | bytes 393220
  4.7 15.4 %all-to-all-start = ((bf16[16,2,2048]{2,1,0:T(2,128)(2,1)}), bf16[16,2,2048]{2,1,0:T(2,128)(2,1)S(1)}, u32[]{:S(2)}, u32[]{:S(2)}) async-start(bf16[16,2,2048]{2,1,0:T(2,128)(2,1)} %reshape.50), calls=%async_computation | async-start | bytes 262144 | tf_op jit(solution)/shard_map/all_to_all | solution.py:62
  13.1 11.6 %copy-start.4 = (f32[64]{0:T(128)S(1)}, f32[64]{0:T(128)}, u32[]{:S(2)}) copy-start(f32[64]{0:T(128)} %param.22) | copy-start | bytes 772
  13.4 21.6 %copy-start.6 = (s32[256]{0:T(256)S(1)}, s32[256]{0:T(256)}, u32[]{:S(2)}) copy-start(s32[256]{0:T(256)} %param.25) | copy-start | bytes 3076
  20.1 11.4 %all-to-all-start.1 = ((bf16[16,2,2048]{2,1,0:T(2,128)(2,1)}), bf16[16,2,2048]{2,1,0:T(2,128)(2,1)S(1)}, u32[]{:S(2)}, u32[]{:S(2)}) async-start(bf16[16,2,2048]{2,1,0:T(2,128)(2,1)} %reshape.52), calls=%async_computation.1 | async-start | bytes 262144 | tf_op jit(solution)/shard_map/all_to_all | solution.py:63
  31.5 13.5 %all-to-all-start.2 = ((bf16[16,2,2048]{2,1,0:T(2,128)(2,1)}), bf16[16,2,2048]{2,1,0:T(2,128)(2,1)S(1)}, u32[]{:S(2)}, u32[]{:S(2)}) async-start(bf16[16,2,2048]{2,1,0:T(2,128)(2,1)} %reshape.54), calls=%async_computation.2 | async-start | bytes 262144 | tf_op jit(solution)/shard_map/all_to_all | solution.py:64
  45.2 8.6 %copy-start.5 = (f32[64]{0:T(128)S(1)}, f32[64]{0:T(128)}, u32[]{:S(2)}) copy-start(f32[64]{0:T(128)} %param.23) | copy-start | bytes 772
  62.3 13.6 %all-to-all-start.3 = ((bf16[16,2,2048]{2,1,0:T(2,128)(2,1)}), bf16[16,2,2048]{2,1,0:T(2,128)(2,1)S(1)}, u32[]{:S(2)}, u32[]{:S(2)}) async-start(bf16[16,2,2048]{2,1,0:T(2,128)(2,1)} %reshape.56), calls=%async_computation.3 | async-start | bytes 262144 | tf_op jit(solution)/shard_map/all_to_all | solution.py:112
where the time goes:
time: 77.6 us; the launch traced here: 76.9 us
  starting transfers between devices  20.1 us (26%)
  waiting for transfers between devices  18.5 us (24%)
  blocking collectives  17.5 us (23%)
  local copies, waits for them, and re-layouts  7.24 us (9%)
  other arithmetic  6.54 us (8%)
  matrix products  5.96 us (8%)
  between operations  1 us (1%)
    all_gather x1, blocking collectives, on_device(): lax.all_gather(k_local, 'uly', axis=0, tiled=True)  9.16 us
    all_gather x1, blocking collectives, on_device(): lax.all_gather(v_local, 'uly', axis=0, tiled=True)  8.31 us
    all_to_all x1, starting transfers between devices, on_device(): lax.all_to_all(q_norm, 'blk', split_axis=1, concat_axis=0, tiled=True)  7.45 us
    all_to_all x1, waiting for transfers between devices, on_device(): lax.all_to_all(attended[:video_rows], 'blk', split_axis=0, concat_axis=1,...  7.14 us
    all_to_all x1, waiting for transfers between devices, on_device(): lax.all_to_all(k_norm, 'blk', split_axis=1, concat_axis=0, tiled=True)  6.68 us
    unnamed x25, local copies, waits for them, and re-layouts  6.08 us
    all_to_all x1, starting transfers between devices, on_device(): lax.all_to_all(attended[:video_rows], 'blk', split_axis=0, concat_axis=1,...  5.64 us
    all_to_all x1, waiting for transfers between devices, on_device(): lax.all_to_all(q_norm, 'blk', split_axis=1, concat_axis=0, tiled=True)  4.72 us
  transfers between devices with their start and end apart: 4, of which 3 were waited for; matrix products, arithmetic and copies ran while one was open for 8% of the time, Pallas kernels for 0%

commit v1 on v0

--- a/solution.py
+++ b/solution.py
@@ -1,12 +1,16 @@
+import functools
 import math
 
 import jax
 import jax.numpy as jnp
 from jax import lax
+from jax.experimental import pallas as pl
+from jax.experimental.pallas import tpu as pltpu
 from jax.sharding import PartitionSpec as P
 
 EPSILON = 1e-06
 NEGATIVE = -1e30
+MESH = pl.DeviceIdType.MESH
 
 
 def normed(tensor, gain_vector, rescale_factor):
@@ -114,24 +118,423 @@
     return (vid_out, txt_out)
 
 
+def peer_id(flat, uly_count):
+    return {"blk": flat // uly_count, "uly": flat % uly_count}
+
+
+def lane_mask(shape, half):
+    return lax.broadcasted_iota(jnp.int32, shape, len(shape) - 1) < half
+
+
+def unit_rows(rows):
+    return rows * lax.rsqrt(jnp.mean(rows * rows, axis=-1, keepdims=True) + EPSILON)
+
+
+def fused_kernel(
+    blk_count,
+    uly_count,
+    vq_hbm,
+    vk_hbm,
+    vv_hbm,
+    tq_hbm,
+    tk_hbm,
+    tv_hbm,
+    vq_gain,
+    vk_gain,
+    tq_gain,
+    tk_gain,
+    sharp,
+    valid,
+    vid_out,
+    txt_out,
+    vq_in,
+    vk_in,
+    vv_in,
+    tq_in,
+    tk_in,
+    tv_in,
+    kv_wide,
+    q_wide,
+    text_wide,
+    send,
+    recv,
+    text_kv,
+    values,
+    text_q,
+    back_send,
+    back_recv,
+    back_wide,
+    text_send,
+    text_recv,
+    text_out_wide,
+    in_sem,
+    send_sem,
+    recv_sem,
+    back_send_sem,
+    back_recv_sem,
+    text_send_sem,
+    text_recv_sem,
+):
+    count = blk_count * uly_count
+    my_blk = lax.axis_index("blk")
+    my_uly = lax.axis_index("uly")
+    me = my_blk * uly_count + my_uly
+    tokens, heads, width = vq_in.shape
+    half_tokens = tokens // 2
+    text_tokens, band, _ = tq_in.shape
+    text_share = text_tokens // uly_count
+    lanes = 2 * width
+
+    barrier = pltpu.get_barrier_semaphore()
+
+    def greet(step, carry):
+        peer = (me + 1 + step) % count
+        pl.semaphore_signal(
+            barrier, inc=1, device_id=peer_id(peer, uly_count), device_id_type=MESH
+        )
+        return carry
+
+    lax.fori_loop(0, count - 1, greet, 0)
+
+    band_start = pl.multiple_of(me // band * band, band)
+    loads = []
+    for slot, (source, target) in enumerate(
+        ((vk_hbm, vk_in), (vv_hbm, vv_in), (vq_hbm, vq_in))
+    ):
+        loads.append(pltpu.make_async_copy(source, target, in_sem.at[slot]))
+    for slot, (source, target) in enumerate(
+        ((tk_hbm, tk_in), (tv_hbm, tv_in), (tq_hbm, tq_in))
+    ):
+        loads.append(
+            pltpu.make_async_copy(
+                source.at[:, pl.ds(band_start, band), :], target, in_sem.at[3 + slot]
+            )
+        )
+    for load in loads:
+        load.start()
+
+    sharp_row = sharp[...] / math.sqrt(width)
+    square = (heads, heads)
+    sharp_column = jnp.sum(
+        jnp.where(
+            lax.broadcasted_iota(jnp.int32, square, 0) == lax.broadcasted_iota(jnp.int32, square, 1),
+            jnp.broadcast_to(sharp_row, square),
+            0.0,
+        ),
+        axis=1,
+        keepdims=True,
+    )
+    my_sharp = jnp.sum(
+        jnp.where(lax.broadcasted_iota(jnp.int32, (1, heads), 1) == me, sharp_row, 0.0),
+        axis=1,
+        keepdims=True,
+    )
+
+    loads[0].wait()
+    loads[1].wait()
+    keys = unit_rows(vk_in[...].astype(jnp.float32)) * vk_gain[...][None]
+    kv_wide[...] = jnp.concatenate([keys, vv_in[...].astype(jnp.float32)], axis=-1)
+    loads[2].wait()
+    probes = unit_rows(vq_in[...].astype(jnp.float32)) * vq_gain[...][None] * sharp_column[None]
+    q_wide[...] = jnp.concatenate([probes[:half_tokens], probes[half_tokens:]], axis=-1)
+    for head in range(heads):
+        send[head, :tokens, :] = kv_wide[:, head, :].astype(jnp.bfloat16)
+        send[head, tokens:, :] = q_wide[:, head, :].astype(jnp.bfloat16)
+    recv[me] = send[me]
+
+    pl.semaphore_wait(barrier, count - 1)
+
+    def outward(peer):
+        return pltpu.make_async_remote_copy(
+            src_ref=send.at[peer],
+            dst_ref=recv.at[me],
+            send_sem=send_sem.at[peer],
+            recv_sem=recv_sem.at[me],
+            device_id=peer_id(peer, uly_count),
+            device_id_type=MESH,
+        )
+
+    def inward(peer):
+        return pltpu.make_async_remote_copy(
+            src_ref=send.at[peer],
+            dst_ref=recv.at[peer],
+            send_sem=send_sem.at[peer],
+            recv_sem=recv_sem.at[peer],
+            device_id=peer_id(peer, uly_count),
+            device_id_type=MESH,
+        )
+
+    def dispatch(step, carry):
+        distance = count // 2 + (1 - 2 * (step % 2)) * ((step + 1) // 2)
+        outward((me + distance) % count).start()
+        return carry
+
+    lax.fori_loop(0, count - 1, dispatch, 0)
+
+    my_row = me % band
+    loads[3].wait()
+    text_wide[...] = tk_in[...].astype(jnp.float32)
+    text_keys = unit_rows(text_wide[:, my_row, :]) * tk_gain[...]
+    loads[4].wait()
+    text_wide[...] = tv_in[...].astype(jnp.float32)
+    both = jnp.concatenate([text_keys, text_wide[:, my_row, :]], axis=-1)
+    text_kv[...] = both.astype(jnp.bfloat16)
+    video_tokens = count * tokens
+    values[video_tokens:, :] = jnp.where(lane_mask(both.shape, width), 1.0, both).astype(
+        jnp.bfloat16
+    )
+    loads[5].wait()
+    text_wide[...] = tq_in[...].astype(jnp.float32)
+    text_probes = unit_rows(text_wide[:, my_row, :]) * tq_gain[...] * my_sharp
+    text_q[...] = jnp.concatenate([text_probes, jnp.zeros_like(text_probes)], axis=-1).astype(
+        jnp.bfloat16
+    )
+    bias = jnp.where(valid[...] == 1, 0.0, NEGATIVE)
+
+    def arrive(step, carry):
+        inward((me + 1 + step) % count).wait_recv()
+        return carry
+
+    lax.fori_loop(0, count - 1, arrive, 0)
+
+    video_kv = recv[:, :tokens, :].reshape(video_tokens, lanes)
+    values[:video_tokens, :] = jnp.where(
+        lane_mask(video_kv.shape, width), 1.0, video_kv.astype(jnp.float32)
+    ).astype(jnp.bfloat16)
+
+    def attend(rows):
+        video_scores = lax.dot_general(
+            rows,
+            recv[:, :tokens, :].reshape(video_tokens, lanes),
+            (((1,), (1,)), ((), ())),
+            preferred_element_type=jnp.float32,
+        )
+        text_scores = (
+            lax.dot_general(
+                rows,
+                text_kv[...],
+                (((1,), (1,)), ((), ())),
+                preferred_element_type=jnp.float32,
+            )
+            + bias
+        )
+        peak = jnp.maximum(
+            jnp.max(video_scores, axis=1, keepdims=True),
+            jnp.max(text_scores, axis=1, keepdims=True),
+        )
+        video_weights = jnp.exp(video_scores - peak).astype(jnp.bfloat16)
+        text_weights = jnp.exp(text_scores - peak).astype(jnp.bfloat16)
+        total = jnp.dot(
+            video_weights, values[:video_tokens, :], preferred_element_type=jnp.float32
+        ) + jnp.dot(text_weights, values[video_tokens:, :], preferred_element_type=jnp.float32)
+        return total / pltpu.roll(total, width, 1)
+
+    def pair_up(first, second):
+        return jnp.where(lane_mask(first.shape, width), pltpu.roll(first, width, 1), second)
+
+    def homeward(peer):
+        return pltpu.make_async_remote_copy(
+            src_ref=back_send.at[peer],
+            dst_ref=back_recv.at[me],
+            send_sem=back_send_sem.at[peer],
+            recv_sem=back_recv_sem.at[me],
+            device_id=peer_id(peer, uly_count),
+            device_id_type=MESH,
+        )
+
+    def returned(peer):
+        return pltpu.make_async_remote_copy(
+            src_ref=back_send.at[peer],
+            dst_ref=back_recv.at[peer],
+            send_sem=back_send_sem.at[peer],
+            recv_sem=back_recv_sem.at[peer],
+            device_id=peer_id(peer, uly_count),
+            device_id_type=MESH,
+        )
+
+    group = math.gcd(count, 8)
+    group_count = count // group
+    group_rows = group * half_tokens
+
+    def video_group(step, carry):
+        which = (me // group + group_count // 2 + step) % group_count
+        first_peer = pl.multiple_of(which * group, group)
+        packed = (
+            recv[pl.ds(first_peer, group), tokens:, :]
+            .reshape(group_rows, lanes)
+            .astype(jnp.float32)
+        )
+        low = lane_mask(packed.shape, width)
+        rows = jnp.concatenate(
+            [jnp.where(low, packed, 0.0), jnp.where(low, pltpu.roll(packed, width, 1), 0.0)], axis=0
+        ).astype(jnp.bfloat16)
+        attended = attend(rows)
+        back_send[pl.ds(first_peer, group)] = (
+            pair_up(attended[:group_rows], attended[group_rows:])
+            .astype(jnp.bfloat16)
+            .reshape(group, half_tokens, lanes)
+        )
+
+        def hand_back(index, inner):
+            peer = first_peer + (index + me) % group
+
+            @pl.when(peer != me)
+            def _():
+                homeward(peer).start()
+
+            return inner
+
+        lax.fori_loop(0, group, hand_back, 0)
+        return carry
+
+    lax.fori_loop(0, group_count, video_group, 0)
+    back_recv[me] = back_send[me]
+
+    attended = attend(text_q[...])
+    half_share = text_share // 2
+    for part in range(uly_count):
+        base = part * text_share
+        text_send[part] = pair_up(
+            attended[base : base + half_share], attended[base + half_share : base + text_share]
+        ).astype(jnp.bfloat16)
+
+    def text_copy(part, slot):
+        return pltpu.make_async_remote_copy(
+            src_ref=text_send.at[part],
+            dst_ref=text_recv.at[slot],
+            send_sem=text_send_sem.at[part],
+            recv_sem=text_recv_sem.at[slot],
+            device_id={"blk": my_blk, "uly": part},
+            device_id_type=MESH,
+        )
+
+    for step in range(1, uly_count):
+        text_copy((my_uly + step) % uly_count, my_uly).start()
+    text_recv[my_uly] = text_send[my_uly]
+
+    for step in range(1, uly_count):
+        other = (my_uly + step) % uly_count
+        text_copy(other, other).wait_recv()
+    for part in range(uly_count):
+        block = text_recv[part].astype(jnp.float32)
+        text_out_wide[:, part, :] = jnp.concatenate([block[:, :width], block[:, width:]], axis=0)
+    txt_out[...] = text_out_wide[...].astype(jnp.bfloat16)
+
+    def collect(step, carry):
+        returned((me + 1 + step) % count).wait_recv()
+        return carry
+
+    lax.fori_loop(0, count - 1, collect, 0)
+    for head in range(heads):
+        back_wide[:, head, :] = back_recv[head].astype(jnp.float32)
+    vid_out[:half_tokens] = back_wide[:, :, :width].astype(jnp.bfloat16)
+    vid_out[half_tokens:] = back_wide[:, :, width:].astype(jnp.bfloat16)
+
+    def drain(step, carry):
+        peer = (me + 1 + step) % count
+        outward(peer).wait_send()
+        homeward(peer).wait_send()
+        return carry
+
+    lax.fori_loop(0, count - 1, drain, 0)
+    for step in range(1, uly_count):
+        text_copy((my_uly + step) % uly_count, my_uly).wait_send()
+
+
+def fused_on_device(blk_count, uly_count, *operands):
+    vq, vk, vv, tq, tk, tv, vq_gain, vk_gain, tq_gain, tk_gain, sharp, valid = operands
+    tokens, heads, width = vq.shape
+    text_tokens = tq.shape[0]
+    count = blk_count * uly_count
+    lanes = 2 * width
+    text_share = text_tokens // uly_count
+    band = math.gcd(heads, 8)
+    half = tokens // 2
+    bf16, f32 = jnp.bfloat16, jnp.float32
+    any_spec = pl.BlockSpec(memory_space=pl.ANY)
+    vmem_spec = pl.BlockSpec(memory_space=pltpu.VMEM)
+    dma = pltpu.SemaphoreType.DMA
+    return pl.pallas_call(
+        functools.partial(fused_kernel, blk_count, uly_count),
+        out_shape=(
+            jax.ShapeDtypeStruct((tokens, heads, width), bf16),
+            jax.ShapeDtypeStruct((text_share, uly_count, width), bf16),
+        ),
+        in_specs=[any_spec] * 6 + [vmem_spec] * 6,
+        out_specs=(vmem_spec, vmem_spec),
+        scratch_shapes=[
+            pltpu.VMEM((tokens, heads, width), bf16),
+            pltpu.VMEM((tokens, heads, width), bf16),
+            pltpu.VMEM((tokens, heads, width), bf16),
+            pltpu.VMEM((text_tokens, band, width), bf16),
+            pltpu.VMEM((text_tokens, band, width), bf16),
+            pltpu.VMEM((text_tokens, band, width), bf16),
+            pltpu.VMEM((tokens, heads, lanes), f32),
+            pltpu.VMEM((half, heads, lanes), f32),
+            pltpu.VMEM((text_tokens, band, width), f32),
+            pltpu.VMEM((count, tokens + half, lanes), bf16),
+            pltpu.VMEM((count, tokens + half, lanes), bf16),
+            pltpu.VMEM((text_tokens, lanes), bf16),
+            pltpu.VMEM((count * tokens + text_tokens, lanes), bf16),
+            pltpu.VMEM((text_tokens, lanes), bf16),
+            pltpu.VMEM((count, half, lanes), bf16),
+            pltpu.VMEM((count, half, lanes), bf16),
+            pltpu.VMEM((half, heads, lanes), f32),
+            pltpu.VMEM((uly_count, text_share // 2, lanes), bf16),
+            pltpu.VMEM((uly_count, text_share // 2, lanes), bf16),
+            pltpu.VMEM((text_share, uly_count, width), f32),
+            dma((6,)),
+            dma((count,)),
+            dma((count,)),
+            dma((count,)),
+            dma((count,)),
+            dma((uly_count,)),
+            dma((uly_count,)),
+        ],
+        compiler_params=pltpu.CompilerParams(collective_id=0, has_side_effects=True),
+        name="joint_attention",
+    )(
+        vq,
+        vk,
+        vv,
+        tq,
+        tk,
+        tv,
+        vq_gain[None],
+        vk_gain[None],
+        tq_gain[None],
+        tk_gain[None],
+        sharp[None],
+        valid[None],
+    )
+
+
+def fits_fused(mesh, vq, tq):
+    count = mesh.shape["blk"] * mesh.shape["uly"]
+    tokens = vq.shape[0] // count
+    return (
+        vq.shape[1] == count
+        and 2 * vq.shape[2] == 128
+        and tokens % 32 == 0
+        and tokens <= 64
+        and tq.shape[0] % (32 * mesh.shape["uly"]) == 0
+    )
+
+
 def solution(mesh):
-    return jax.shard_map(
-        on_device,
-        mesh=mesh,
-        in_specs=(
-            P(("blk", "uly"), None, None),
-            P(("blk", "uly"), None, None),
-            P(("blk", "uly"), None, None),
-            P(),
-            P(),
-            P(),
-            P(),
-            P(),
-            P(),
-            P(),
-            P(),
-            P(),
-        ),
-        out_specs=(P(("blk", "uly"), None, None), P("uly", "blk", None)),
-        check_vma=False,
-    )
+    blk_count, uly_count = mesh.shape["blk"], mesh.shape["uly"]
+
+    def run(*operands):
+        body = on_device
+        if fits_fused(mesh, operands[0], operands[3]):
+            body = functools.partial(fused_on_device, blk_count, uly_count)
+        split = P(("blk", "uly"), None, None)
+        return jax.shard_map(
+            body,
+            mesh=mesh,
+            in_specs=(split, split, split) + (P(),) * 9,
+            out_specs=(split, P("uly", "blk", None)),
+            check_vma=False,
+        )(*operands)
+
+    return run

time: 77.6 us -> 46.2 us (0.60)
  Pallas kernels: 0 us -> 29.7 us
  starting transfers between devices: 20.1 us -> 0 us
  waiting for transfers between devices: 18.5 us -> 0 us
  blocking collectives: 17.5 us -> 0 us
  local copies, waits for them, and re-layouts: 7.24 us -> 15.6 us
  other arithmetic: 6.54 us -> 0 us
  matrix products: 5.96 us -> 0 us
    pallas_call x0 -> x1, Pallas kernels: none -> 29.7 us  [fused_on_device(): pl.pallas_call(functools.partial(fused_kernel, blk_count, uly_count), out...]
    all_to_all x4 -> x0, starting transfers between devices: 20.1 us -> none  [the longest x1 7.45 us: on_device(): lax.all_to_all(q_norm, 'blk', split_axis=1, concat_axis=0, tiled=True)]
    all_to_all x4 -> x0, waiting for transfers between devices: 18.5 us -> none  [the longest x1 7.14 us: on_device(): lax.all_to_all(attended[:video_rows], 'blk', split_axis=0, concat_axis=1,...]
    all_gather x2 -> x0, blocking collectives: 17.5 us -> none  [the longest x1 9.16 us: on_device(): lax.all_gather(k_local, 'uly', axis=0, tiled=True)]
    unnamed x25 -> x8, local copies, waits for them, and re-layouts: 6.08 us -> 14.1 us
    dot_general x6 -> x0, matrix products: 5.96 us -> none  [the longest x3 3.51 us: fragment_contributions(): jnp.einsum('hqk,khd->hqd', weights, value_rows.astype(jnp.float32), preci...]
    reduce_sum x6 -> x0, other arithmetic: 3.29 us -> none  [the longest x3 2.3 us: normed(): jnp.mean(widened * widened, axis=-1, keepdims=True) + EPSILON]
    pallas_call x0 -> x1, local copies, waits for them, and re-layouts: none -> 1.55 us  [fused_on_device(): pl.pallas_call(functools.partial(fused_kernel, blk_count, uly_count), out...]
  transfers between devices with their start and end apart: 4 -> 0, of which waited for: 3 -> 0; matrix products, arithmetic and copies ran while one was open for 8% -> 0% of each run, Pallas kernels for 0% -> 0%
where the time goes in v1:
time: 46.2 us; the launch traced here: 46 us
  Pallas kernels  29.7 us (64%)
  local copies, waits for them, and re-layouts  15.6 us (34%)
  between operations  0.65 us (1%)
    pallas_call x1, Pallas kernels, fused_on_device(): pl.pallas_call(functools.partial(fused_kernel, blk_count, uly_count), out...  29.7 us
    unnamed x8, local copies, waits for them, and re-layouts  14.1 us
    pallas_call x1, local copies, waits for them, and re-layouts, fused_on_device(): pl.pallas_call(functools.partial(fused_kernel, blk_count, uly_count), out...  1.55 us

profile of v1, /device:TPU:0, one launch (start us, length us, event | category | flops | bytes accessed | tf_op | source)
XLA Modules:
  0.0 46.0 jit_solution(11804679658103222944)
XLA Ops:
  0.6 0.0 copy-start
  0.6 4.8 %copy.14.tq_hbm = bf16[256,32,64]{2,1,0:T(8,128)(2,1)} copy(bf16[256,32,64]{0,2,1:T(8,128)(2,1)} %param.15) | data formatting | bytes 2097152 | tf_op args[3]
  5.4 0.0 copy-done
  5.4 0.0 copy-start.1
  5.4 3.8 %copy.15.tk_hbm = bf16[256,32,64]{2,1,0:T(8,128)(2,1)} copy(bf16[256,32,64]{0,2,1:T(8,128)(2,1)S(1)} %copy-done) | data formatting | bytes 2097152 | tf_op args[4]
  9.2 0.0 copy-done.1
  9.2 3.8 %copy.16.tv_hbm = bf16[256,32,64]{2,1,0:T(8,128)(2,1)} copy(bf16[256,32,64]{0,2,1:T(8,128)(2,1)S(1)} %copy-done.1) | data formatting | bytes 2097152 | tf_op args[5]
  13.1 29.7 %joint_attention.1 = (bf16[32,32,64]{2,1,0:T(8,128)(2,1)}, bf16[128,2,64]{2,1,0:T(2,128)(2,1)}) custom-call(bf16[32,32,64]{2,1,0:T(8,128)(2,1)} %vq_hbm.1, bf16[32,32,64]{2,1,0:T(8,128)(2,1)} %vk_hbm.1, bf16[32,32,64]{2,1,0:T(8,128)(2,1)} %vv_hbm.1, bf16[256,32,64]{2,1,0:T(8,128)(2,1)} %copy.14.tq_hbm, bf16[256,32,64]{2,1,0:T(8,128)(2,1)} %copy.15.tk_hbm, ...), custom_call_target="tpu_custom_call" | custom-call | tf_op jit(solution)/shard_map/joint_attention/pallas_call | solution.py:457
  42.8 1.6 %copy.17 = bf16[128,2,64]{0,2,1:T(8,128)(2,1)} copy(bf16[128,2,64]{2,1,0:T(2,128)(2,1)} %get-tuple-element.3) | data formatting | bytes 65536 | tf_op jit(solution)/shard_map/joint_attention/pallas_call | solution.py:457
  44.3 1.7 %copy.19 = bf16[32,32,64]{2,1,0:T(8,128)(2,1)} copy(bf16[32,32,64]{2,1,0:T(8,128)(2,1)} %get-tuple-element.6) | data formatting | bytes 262144
Async XLA Ops:
  0.6 4.8 %copy-start = (bf16[256,32,64]{0,2,1:T(8,128)(2,1)S(1)}, bf16[256,32,64]{0,2,1:T(8,128)(2,1)}, u32[]{:S(2)}) copy-start(bf16[256,32,64]{0,2,1:T(8,128)(2,1)} %param.16) | copy-start | bytes 3145732
  5.4 3.8 %copy-start.1 = (bf16[256,32,64]{0,2,1:T(8,128)(2,1)S(1)}, bf16[256,32,64]{0,2,1:T(8,128)(2,1)}, u32[]{:S(2)}) copy-start(bf16[256,32,64]{0,2,1:T(8,128)(2,1)} %param.17) | copy-start | bytes 3145732

commit v2 on v1

--- a/solution.py
+++ b/solution.py
@@ -155,7 +155,6 @@
     tv_in,
     kv_wide,
     q_wide,
-    text_wide,
     send,
     recv,
     text_kv,
@@ -166,7 +165,6 @@
     back_wide,
     text_send,
     text_recv,
-    text_out_wide,
     in_sem,
     send_sem,
     recv_sem,
@@ -181,7 +179,7 @@
     me = my_blk * uly_count + my_uly
     tokens, heads, width = vq_in.shape
     half_tokens = tokens // 2
-    text_tokens, band, _ = tq_in.shape
+    _, text_tokens = tq_in.shape
     text_share = text_tokens // uly_count
     lanes = 2 * width
 
@@ -196,7 +194,6 @@
 
     lax.fori_loop(0, count - 1, greet, 0)
 
-    band_start = pl.multiple_of(me // band * band, band)
     loads = []
     for slot, (source, target) in enumerate(
         ((vk_hbm, vk_in), (vv_hbm, vv_in), (vq_hbm, vq_in))
@@ -206,9 +203,7 @@
         ((tk_hbm, tk_in), (tv_hbm, tv_in), (tq_hbm, tq_in))
     ):
         loads.append(
-            pltpu.make_async_copy(
-                source.at[:, pl.ds(band_start, band), :], target, in_sem.at[3 + slot]
-            )
+            pltpu.make_async_copy(source.at[me], target, in_sem.at[3 + slot])
         )
     for load in loads:
         load.start()
@@ -271,21 +266,21 @@
 
     lax.fori_loop(0, count - 1, dispatch, 0)
 
-    my_row = me % band
+    def text_columns(text_in):
+        return text_in[...].astype(jnp.float32).T
+
     loads[3].wait()
-    text_wide[...] = tk_in[...].astype(jnp.float32)
-    text_keys = unit_rows(text_wide[:, my_row, :]) * tk_gain[...]
     loads[4].wait()
-    text_wide[...] = tv_in[...].astype(jnp.float32)
-    both = jnp.concatenate([text_keys, text_wide[:, my_row, :]], axis=-1)
+    both = jnp.concatenate(
+        [unit_rows(text_columns(tk_in)) * tk_gain[...], text_columns(tv_in)], axis=-1
+    )
     text_kv[...] = both.astype(jnp.bfloat16)
     video_tokens = count * tokens
     values[video_tokens:, :] = jnp.where(lane_mask(both.shape, width), 1.0, both).astype(
         jnp.bfloat16
     )
     loads[5].wait()
-    text_wide[...] = tq_in[...].astype(jnp.float32)
-    text_probes = unit_rows(text_wide[:, my_row, :]) * tq_gain[...] * my_sharp
+    text_probes = unit_rows(text_columns(tq_in)) * tq_gain[...] * my_sharp
     text_q[...] = jnp.concatenate([text_probes, jnp.zeros_like(text_probes)], axis=-1).astype(
         jnp.bfloat16
     )
@@ -391,12 +386,11 @@
     back_recv[me] = back_send[me]
 
     attended = attend(text_q[...])
-    half_share = text_share // 2
+    turned = attended.T[width:]
     for part in range(uly_count):
-        base = part * text_share
-        text_send[part] = pair_up(
-            attended[base : base + half_share], attended[base + half_share : base + text_share]
-        ).astype(jnp.bfloat16)
+        text_send[part] = turned[:, part * text_share : (part + 1) * text_share].astype(
+            jnp.bfloat16
+        )
 
     def text_copy(part, slot):
         return pltpu.make_async_remote_copy(
@@ -415,10 +409,7 @@
     for step in range(1, uly_count):
         other = (my_uly + step) % uly_count
         text_copy(other, other).wait_recv()
-    for part in range(uly_count):
-        block = text_recv[part].astype(jnp.float32)
-        text_out_wide[:, part, :] = jnp.concatenate([block[:, :width], block[:, width:]], axis=0)
-    txt_out[...] = text_out_wide[...].astype(jnp.bfloat16)
+    txt_out[...] = text_recv[...]
 
     def collect(step, carry):
         returned((me + 1 + step) % count).wait_recv()
@@ -448,17 +439,16 @@
     count = blk_count * uly_count
     lanes = 2 * width
     text_share = text_tokens // uly_count
-    band = math.gcd(heads, 8)
     half = tokens // 2
     bf16, f32 = jnp.bfloat16, jnp.float32
     any_spec = pl.BlockSpec(memory_space=pl.ANY)
     vmem_spec = pl.BlockSpec(memory_space=pltpu.VMEM)
     dma = pltpu.SemaphoreType.DMA
-    return pl.pallas_call(
+    vid_out, txt_out = pl.pallas_call(
         functools.partial(fused_kernel, blk_count, uly_count),
         out_shape=(
             jax.ShapeDtypeStruct((tokens, heads, width), bf16),
-            jax.ShapeDtypeStruct((text_share, uly_count, width), bf16),
+            jax.ShapeDtypeStruct((uly_count, width, text_share), bf16),
         ),
         in_specs=[any_spec] * 6 + [vmem_spec] * 6,
         out_specs=(vmem_spec, vmem_spec),
@@ -466,12 +456,11 @@
             pltpu.VMEM((tokens, heads, width), bf16),
             pltpu.VMEM((tokens, heads, width), bf16),
             pltpu.VMEM((tokens, heads, width), bf16),
-            pltpu.VMEM((text_tokens, band, width), bf16),
-            pltpu.VMEM((text_tokens, band, width), bf16),
-            pltpu.VMEM((text_tokens, band, width), bf16),
+            pltpu.VMEM((width, text_tokens), bf16),
+            pltpu.VMEM((width, text_tokens), bf16),
+            pltpu.VMEM((width, text_tokens), bf16),
             pltpu.VMEM((tokens, heads, lanes), f32),
             pltpu.VMEM((half, heads, lanes), f32),
-            pltpu.VMEM((text_tokens, band, width), f32),
             pltpu.VMEM((count, tokens + half, lanes), bf16),
             pltpu.VMEM((count, tokens + half, lanes), bf16),
             pltpu.VMEM((text_tokens, lanes), bf16),
@@ -480,9 +469,8 @@
             pltpu.VMEM((count, half, lanes), bf16),
             pltpu.VMEM((count, half, lanes), bf16),
             pltpu.VMEM((half, heads, lanes), f32),
-            pltpu.VMEM((uly_count, text_share // 2, lanes), bf16),
-            pltpu.VMEM((uly_count, text_share // 2, lanes), bf16),
-            pltpu.VMEM((text_share, uly_count, width), f32),
+            pltpu.VMEM((uly_count, width, text_share), bf16),
+            pltpu.VMEM((uly_count, width, text_share), bf16),
             dma((6,)),
             dma((count,)),
             dma((count,)),
@@ -497,9 +485,9 @@
         vq,
         vk,
         vv,
-        tq,
-        tk,
-        tv,
+        jnp.transpose(tq, (1, 2, 0)),
+        jnp.transpose(tk, (1, 2, 0)),
+        jnp.transpose(tv, (1, 2, 0)),
         vq_gain[None],
         vk_gain[None],
         tq_gain[None],
@@ -507,6 +495,7 @@
         sharp[None],
         valid[None],
     )
+    return vid_out, jnp.transpose(txt_out, (2, 0, 1))
 
 
 def fits_fused(mesh, vq, tq):
@@ -517,7 +506,7 @@
         and 2 * vq.shape[2] == 128
         and tokens % 32 == 0
         and tokens <= 64
-        and tq.shape[0] % (32 * mesh.shape["uly"]) == 0
+        and tq.shape[0] % (128 * mesh.shape["uly"]) == 0
     )
 
 

time: 46.2 us -> 33.1 us (0.72)
  local copies, waits for them, and re-layouts: 15.6 us -> 2.29 us
    unnamed x8 -> x4, local copies, waits for them, and re-layouts: 14.1 us -> 2.29 us
    pallas_call x1 -> x0, local copies, waits for them, and re-layouts: 1.55 us -> none  [fused_on_device(): pl.pallas_call(functools.partial(fused_kernel, blk_count, uly_count), out...]
where the time goes in v2:
time: 33.1 us; the launch traced here: 33 us
  Pallas kernels  30 us (91%)
  local copies, waits for them, and re-layouts  2.29 us (7%)
  between operations  0.65 us (2%)
    pallas_call x1, Pallas kernels, fused_on_device(): pl.pallas_call(functools.partial(fused_kernel, blk_count, uly_count), out...  30 us
    unnamed x4, local copies, waits for them, and re-layouts  2.29 us

profile of v2, /device:TPU:0, one launch (start us, length us, event | category | flops | bytes accessed | tf_op | source)
XLA Modules:
  0.0 33.0 jit_solution(4154320341220519114)
XLA Ops:
  0.6 30.0 %joint_attention.1 = (bf16[32,32,64]{2,1,0:T(8,128)(2,1)}, bf16[2,64,128]{2,1,0:T(8,128)(2,1)}) custom-call(bf16[32,32,64]{2,1,0:T(8,128)(2,1)} %vq_hbm.1, bf16[32,32,64]{2,1,0:T(8,128)(2,1)} %vk_hbm.1, bf16[32,32,64]{2,1,0:T(8,128)(2,1)} %vv_hbm.1, bf16[32,64,256]{2,1,0:T(8,128)(2,1)} %bitcast.10, bf16[32,64,256]{2,1,0:T(8,128)(2,1)} %bitcast.11, ...), custom_call_target="tpu_custom_call" | custom-call | tf_op jit(solution)/shard_map/joint_attention/pallas_call | solution.py:447
  30.7 0.0 copy-start
  30.7 1.7 %copy.16 = bf16[32,32,64]{2,1,0:T(8,128)(2,1)} copy(bf16[32,32,64]{2,1,0:T(8,128)(2,1)} %get-tuple-element.8) | data formatting | bytes 262144
  32.4 0.0 copy-done
  32.4 0.6 %copy.17 = bf16[128,2,64]{0,2,1:T(8,128)(2,1)} copy(bf16[128,2,64]{0,2,1:T(8,128)(2,1)S(1)} %bitcast.13) | data formatting | bytes 65536
Async XLA Ops:
  30.7 1.7 %copy-start = (bf16[2,64,128]{2,1,0:T(8,128)(2,1)S(1)}, bf16[2,64,128]{2,1,0:T(8,128)(2,1)}, u32[]{:S(2)}) copy-start(bf16[2,64,128]{2,1,0:T(8,128)(2,1)} %get-tuple-element.5) | copy-start | bytes 98308

commit v3 on v2

--- a/solution.py
+++ b/solution.py
@@ -145,7 +145,7 @@
     tk_gain,
     sharp,
     valid,
-    vid_out,
+    back_out,
     txt_out,
     vq_in,
     vk_in,
@@ -158,14 +158,16 @@
     send,
     recv,
     text_kv,
-    values,
-    text_q,
+    queries,
+    totals,
+    peaks,
     back_send,
     back_recv,
-    back_wide,
     text_send,
     text_recv,
     in_sem,
+    q_send_sem,
+    q_recv_sem,
     send_sem,
     recv_sem,
     back_send_sem,
@@ -239,32 +241,56 @@
 
     pl.semaphore_wait(barrier, count - 1)
 
-    def outward(peer):
+    query_part, kv_part = pl.ds(tokens, half_tokens), pl.ds(0, tokens)
+
+    def outward(peer, part, sent, landed):
         return pltpu.make_async_remote_copy(
-            src_ref=send.at[peer],
-            dst_ref=recv.at[me],
-            send_sem=send_sem.at[peer],
-            recv_sem=recv_sem.at[me],
+            src_ref=send.at[peer, part],
+            dst_ref=recv.at[me, part],
+            send_sem=sent.at[peer],
+            recv_sem=landed.at[me],
             device_id=peer_id(peer, uly_count),
             device_id_type=MESH,
         )
 
-    def inward(peer):
+    def inward(peer, part, sent, landed):
         return pltpu.make_async_remote_copy(
-            src_ref=send.at[peer],
-            dst_ref=recv.at[peer],
-            send_sem=send_sem.at[peer],
-            recv_sem=recv_sem.at[peer],
+            src_ref=send.at[peer, part],
+            dst_ref=recv.at[peer, part],
+            send_sem=sent.at[peer],
+            recv_sem=landed.at[peer],
             device_id=peer_id(peer, uly_count),
             device_id_type=MESH,
         )
 
-    def dispatch(step, carry):
+    def dispatch_queries(step, carry):
         distance = count // 2 + (1 - 2 * (step % 2)) * ((step + 1) // 2)
-        outward((me + distance) % count).start()
+        outward((me + distance) % count, query_part, q_send_sem, q_recv_sem).start()
         return carry
 
-    lax.fori_loop(0, count - 1, dispatch, 0)
+    lax.fori_loop(0, count - 1, dispatch_queries, 0)
+
+    group = math.gcd(count, 8)
+    group_count = count // group
+    my_group = me // group
+    if group_count == 4:
+        near = my_group + 1 - 2 * (my_group % 2)
+        planes = [my_group, near, (my_group + 2) % 4, 3 - my_group]
+    else:
+        planes = [(my_group + step) % group_count for step in range(group_count)]
+
+    for plane in planes:
+
+        def dispatch(step, carry, plane=plane):
+            peer = plane * group + (step + me) % group
+
+            @pl.when(peer != me)
+            def _():
+                outward(peer, kv_part, send_sem, recv_sem).start()
+
+            return carry
+
+        lax.fori_loop(0, group, dispatch, 0)
 
     def text_columns(text_in):
         return text_in[...].astype(jnp.float32).T
@@ -275,53 +301,103 @@
         [unit_rows(text_columns(tk_in)) * tk_gain[...], text_columns(tv_in)], axis=-1
     )
     text_kv[...] = both.astype(jnp.bfloat16)
-    video_tokens = count * tokens
-    values[video_tokens:, :] = jnp.where(lane_mask(both.shape, width), 1.0, both).astype(
-        jnp.bfloat16
-    )
     loads[5].wait()
     text_probes = unit_rows(text_columns(tq_in)) * tq_gain[...] * my_sharp
-    text_q[...] = jnp.concatenate([text_probes, jnp.zeros_like(text_probes)], axis=-1).astype(
+    block = group * tokens
+    queries[count * tokens :, :] = jnp.concatenate([text_probes, jnp.zeros_like(text_probes)], axis=-1).astype(
         jnp.bfloat16
     )
     bias = jnp.where(valid[...] == 1, 0.0, NEGATIVE)
 
-    def arrive(step, carry):
-        inward((me + 1 + step) % count).wait_recv()
+    def with_ones(pairs):
+        return jnp.where(lane_mask(pairs.shape, width), 1.0, pairs.astype(jnp.float32)).astype(
+            jnp.bfloat16
+        )
+
+    def scores_of(rows, pairs):
+        return lax.dot_general(
+            rows, pairs, (((1,), (1,)), ((), ())), preferred_element_type=jnp.float32
+        )
+
+    def row_max(scores):
+        return jnp.max(scores, axis=1, keepdims=True)
+
+    def weighted(scores, peak, pairs):
+        return jnp.dot(
+            jnp.exp(scores - peak).astype(jnp.bfloat16), pairs, preferred_element_type=jnp.float32
+        )
+
+    def arrive_queries(step, carry):
+        inward((me + 1 + step) % count, query_part, q_send_sem, q_recv_sem).wait_recv()
         return carry
 
-    lax.fori_loop(0, count - 1, arrive, 0)
-
-    video_kv = recv[:, :tokens, :].reshape(video_tokens, lanes)
-    values[:video_tokens, :] = jnp.where(
-        lane_mask(video_kv.shape, width), 1.0, video_kv.astype(jnp.float32)
-    ).astype(jnp.bfloat16)
-
-    def attend(rows):
-        video_scores = lax.dot_general(
-            rows,
-            recv[:, :tokens, :].reshape(video_tokens, lanes),
-            (((1,), (1,)), ((), ())),
-            preferred_element_type=jnp.float32,
-        )
-        text_scores = (
-            lax.dot_general(
-                rows,
-                text_kv[...],
-                (((1,), (1,)), ((), ())),
-                preferred_element_type=jnp.float32,
-            )
-            + bias
-        )
-        peak = jnp.maximum(
-            jnp.max(video_scores, axis=1, keepdims=True),
-            jnp.max(text_scores, axis=1, keepdims=True),
-        )
-        video_weights = jnp.exp(video_scores - peak).astype(jnp.bfloat16)
-        text_weights = jnp.exp(text_scores - peak).astype(jnp.bfloat16)
-        total = jnp.dot(
-            video_weights, values[:video_tokens, :], preferred_element_type=jnp.float32
-        ) + jnp.dot(text_weights, values[video_tokens:, :], preferred_element_type=jnp.float32)
+    lax.fori_loop(0, count - 1, arrive_queries, 0)
+    group_rows = group * half_tokens
+    for index in range(group_count):
+        packed = (
+            recv[index * group : (index + 1) * group, tokens:, :]
+            .reshape(group_rows, lanes)
+            .astype(jnp.float32)
+        )
+        low = lane_mask(packed.shape, width)
+        for side, rows in enumerate((packed, pltpu.roll(packed, width, 1))):
+            start = index * block + side * group_rows
+            queries[start : start + group_rows, :] = jnp.where(low, rows, 0.0).astype(jnp.bfloat16)
+
+    def plane_pairs(plane):
+        def arrive(step, carry):
+            peer = plane * group + step
+
+            @pl.when(peer != me)
+            def _():
+                inward(peer, kv_part, send_sem, recv_sem).wait_recv()
+
+            return carry
+
+        lax.fori_loop(0, group, arrive, 0)
+        first = pl.multiple_of(plane * group, group)
+        return recv[pl.ds(first, group), :tokens, :].reshape(block, lanes)
+
+    block_count = group_count + text_tokens // block
+
+    def block_rows(index):
+        return pl.ds(pl.multiple_of(index * block, block), block)
+
+    text_ones = with_ones(text_kv[...])
+    pairs = plane_pairs(planes[0])
+    ones = with_ones(pairs)
+    for index in range(block_count):
+        rows = queries[block_rows(index), :]
+        scores = scores_of(rows, pairs)
+        text_scores = scores_of(rows, text_kv[...]) + bias
+        peak = jnp.maximum(row_max(scores), row_max(text_scores))
+        totals[block_rows(index), :] = weighted(scores, peak, ones) + weighted(
+            text_scores, peak, text_ones
+        )
+        peaks[block_rows(index), :] = peak
+
+    def absorb(index, pairs, ones):
+        scores = scores_of(queries[block_rows(index), :], pairs)
+        earlier = peaks[block_rows(index), :]
+        peak = jnp.maximum(earlier, row_max(scores))
+        total = totals[block_rows(index), :] * jnp.exp(earlier - peak) + weighted(
+            scores, peak, ones
+        )
+        return peak, total
+
+    for plane in planes[1:-1]:
+        pairs = plane_pairs(plane)
+        ones = with_ones(pairs)
+        for index in range(block_count):
+            peak, total = absorb(index, pairs, ones)
+            totals[block_rows(index), :] = total
+            peaks[block_rows(index), :] = peak
+
+    pairs = plane_pairs(planes[-1])
+    ones = with_ones(pairs)
+
+    def attend(index):
+        _, total = absorb(index, pairs, ones)
         return total / pltpu.roll(total, width, 1)
 
     def pair_up(first, second):
@@ -347,45 +423,30 @@
             device_id_type=MESH,
         )
 
-    group = math.gcd(count, 8)
-    group_count = count // group
-    group_rows = group * half_tokens
-
-    def video_group(step, carry):
-        which = (me // group + group_count // 2 + step) % group_count
+    for which in planes[::-1]:
         first_peer = pl.multiple_of(which * group, group)
-        packed = (
-            recv[pl.ds(first_peer, group), tokens:, :]
-            .reshape(group_rows, lanes)
-            .astype(jnp.float32)
-        )
-        low = lane_mask(packed.shape, width)
-        rows = jnp.concatenate(
-            [jnp.where(low, packed, 0.0), jnp.where(low, pltpu.roll(packed, width, 1), 0.0)], axis=0
-        ).astype(jnp.bfloat16)
-        attended = attend(rows)
+        attended = attend(which)
         back_send[pl.ds(first_peer, group)] = (
             pair_up(attended[:group_rows], attended[group_rows:])
             .astype(jnp.bfloat16)
             .reshape(group, half_tokens, lanes)
         )
 
-        def hand_back(index, inner):
-            peer = first_peer + (index + me) % group
+        def hand_back(step, carry, first_peer=first_peer):
+            peer = first_peer + (step + me) % group
 
             @pl.when(peer != me)
             def _():
                 homeward(peer).start()
 
-            return inner
+            return carry
 
         lax.fori_loop(0, group, hand_back, 0)
-        return carry
-
-    lax.fori_loop(0, group_count, video_group, 0)
     back_recv[me] = back_send[me]
 
-    attended = attend(text_q[...])
+    attended = jnp.concatenate(
+        [attend(index) for index in range(group_count, block_count)], axis=0
+    )
     turned = attended.T[width:]
     for part in range(uly_count):
         text_send[part] = turned[:, part * text_share : (part + 1) * text_share].astype(
@@ -416,20 +477,28 @@
         return carry
 
     lax.fori_loop(0, count - 1, collect, 0)
-    for head in range(heads):
-        back_wide[:, head, :] = back_recv[head].astype(jnp.float32)
-    vid_out[:half_tokens] = back_wide[:, :, :width].astype(jnp.bfloat16)
-    vid_out[half_tokens:] = back_wide[:, :, width:].astype(jnp.bfloat16)
+    back_out[...] = back_recv[...]
 
     def drain(step, carry):
         peer = (me + 1 + step) % count
-        outward(peer).wait_send()
+        outward(peer, query_part, q_send_sem, q_recv_sem).wait_send()
+        outward(peer, kv_part, send_sem, recv_sem).wait_send()
         homeward(peer).wait_send()
         return carry
 
     lax.fori_loop(0, count - 1, drain, 0)
     for step in range(1, uly_count):
         text_copy((my_uly + step) % uly_count, my_uly).wait_send()
+
+
+def lay_out_kernel(back_ref, txt_ref, vid_out, txt_out, wide):
+    heads, half, lanes = back_ref.shape
+    width = lanes // 2
+    for head in range(heads):
+        wide[:, head, :] = back_ref[head].astype(jnp.float32)
+    vid_out[:half] = wide[:, :, :width].astype(jnp.bfloat16)
+    vid_out[half:] = wide[:, :, width:].astype(jnp.bfloat16)
+    txt_out[...] = txt_ref[...]
 
 
 def fused_on_device(blk_count, uly_count, *operands):
@@ -444,11 +513,12 @@
     any_spec = pl.BlockSpec(memory_space=pl.ANY)
     vmem_spec = pl.BlockSpec(memory_space=pltpu.VMEM)
     dma = pltpu.SemaphoreType.DMA
-    vid_out, txt_out = pl.pallas_call(
+    text_shape = jax.ShapeDtypeStruct((uly_count, width, text_share), bf16)
+    back, text_back = pl.pallas_call(
         functools.partial(fused_kernel, blk_count, uly_count),
         out_shape=(
-            jax.ShapeDtypeStruct((tokens, heads, width), bf16),
-            jax.ShapeDtypeStruct((uly_count, width, text_share), bf16),
+            jax.ShapeDtypeStruct((count, half, lanes), bf16),
+            text_shape,
         ),
         in_specs=[any_spec] * 6 + [vmem_spec] * 6,
         out_specs=(vmem_spec, vmem_spec),
@@ -465,13 +535,15 @@
             pltpu.VMEM((count, tokens + half, lanes), bf16),
             pltpu.VMEM((text_tokens, lanes), bf16),
             pltpu.VMEM((count * tokens + text_tokens, lanes), bf16),
-            pltpu.VMEM((text_tokens, lanes), bf16),
+            pltpu.VMEM((count * tokens + text_tokens, lanes), f32),
+            pltpu.VMEM((count * tokens + text_tokens, 1), f32),
             pltpu.VMEM((count, half, lanes), bf16),
             pltpu.VMEM((count, half, lanes), bf16),
-            pltpu.VMEM((half, heads, lanes), f32),
             pltpu.VMEM((uly_count, width, text_share), bf16),
             pltpu.VMEM((uly_count, width, text_share), bf16),
             dma((6,)),
+            dma((count,)),
+            dma((count,)),
             dma((count,)),
             dma((count,)),
             dma((count,)),
@@ -495,6 +567,14 @@
         sharp[None],
         valid[None],
     )
+    vid_out, txt_out = pl.pallas_call(
+        lay_out_kernel,
+        out_shape=(jax.ShapeDtypeStruct((tokens, heads, width), bf16), text_shape),
+        in_specs=[vmem_spec] * 2,
+        out_specs=(vmem_spec, vmem_spec),
+        scratch_shapes=[pltpu.VMEM((half, heads, lanes), f32)],
+        name="lay_out",
+    )(back, text_back)
     return vid_out, jnp.transpose(txt_out, (2, 0, 1))
 
 
@@ -506,6 +586,7 @@
         and 2 * vq.shape[2] == 128
         and tokens % 32 == 0
         and tokens <= 64
+        and tq.shape[0] % (math.gcd(count, 8) * tokens) == 0
         and tq.shape[0] % (128 * mesh.shape["uly"]) == 0
     )
 

time: 33.1 us -> 32.4 us (0.979)
  local copies, waits for them, and re-layouts: 2.29 us -> 0 us
  Pallas kernels: 30 us -> 31.6 us
    unnamed x4 -> x0, local copies, waits for them, and re-layouts: 2.29 us -> none
    pallas_call x0 -> x1, Pallas kernels: none -> 1.96 us  [fused_on_device(): pl.pallas_call(lay_out_kernel, out_shape=(jax.ShapeDtypeStruct((tokens, h...]
    pallas_call x1, Pallas kernels: 30 us -> 29.7 us  [fused_on_device(): pl.pallas_call(functools.partial(fused_kernel, blk_count, uly_count), out...]
where the time goes in v3:
time: 32.4 us; the launch traced here: 32.3 us
  Pallas kernels  31.6 us (98%)
  between operations  0.64 us (2%)
    pallas_call x1, Pallas kernels, fused_on_device(): pl.pallas_call(functools.partial(fused_kernel, blk_count, uly_count), out...  29.7 us
    pallas_call x1, Pallas kernels, fused_on_device(): pl.pallas_call(lay_out_kernel, out_shape=(jax.ShapeDtypeStruct((tokens, h...  1.96 us

profile of v3, /device:TPU:0, one launch (start us, length us, event | category | flops | bytes accessed | tf_op | source)
XLA Modules:
  0.0 32.3 jit_solution(5452811205890029448)
XLA Ops:
  0.6 29.7 %joint_attention.1 = (bf16[32,16,128]{2,1,0:T(8,128)(2,1)}, bf16[2,64,128]{2,1,0:T(8,128)(2,1)}) custom-call(bf16[32,32,64]{2,1,0:T(8,128)(2,1)} %vq_hbm.1, bf16[32,32,64]{2,1,0:T(8,128)(2,1)} %vk_hbm.1, bf16[32,32,64]{2,1,0:T(8,128)(2,1)} %vv_hbm.1, bf16[32,64,256]{2,1,0:T(8,128)(2,1)} %bitcast.10, bf16[32,64,256]{2,1,0:T(8,128)(2,1)} %bitcast.11, ...), custom_call_target="tpu_custom_call" | custom-call | tf_op jit(solution)/shard_map/joint_attention/pallas_call | solution.py:517
  30.3 2.0 %lay_out.1 = (bf16[32,32,64]{2,1,0:T(8,128)(2,1)}, bf16[2,64,128]{2,1,0:T(8,128)(2,1)}) custom-call(bf16[32,16,128]{2,1,0:T(8,128)(2,1)} %get-tuple-element.6.back_ref, bf16[2,64,128]{2,1,0:T(8,128)(2,1)} %get-tuple-element.7.txt_ref), custom_call_target="tpu_custom_call" | custom-call | tf_op jit(solution)/shard_map/lay_out/pallas_call | solution.py:570

commit v4 on v3

--- a/solution.py
+++ b/solution.py
@@ -139,12 +139,12 @@
     tq_hbm,
     tk_hbm,
     tv_hbm,
-    vq_gain,
-    vk_gain,
-    tq_gain,
-    tk_gain,
-    sharp,
-    valid,
+    vq_gain_hbm,
+    vk_gain_hbm,
+    tq_gain_hbm,
+    tk_gain_hbm,
+    sharp_hbm,
+    valid_hbm,
     back_out,
     txt_out,
     vq_in,
@@ -153,6 +153,12 @@
     tq_in,
     tk_in,
     tv_in,
+    vq_gain,
+    vk_gain,
+    tq_gain,
+    tk_gain,
+    sharp,
+    valid,
     kv_wide,
     q_wide,
     send,
@@ -162,10 +168,9 @@
     totals,
     peaks,
     back_send,
-    back_recv,
     text_send,
-    text_recv,
     in_sem,
+    own_sem,
     q_send_sem,
     q_recv_sem,
     send_sem,
@@ -188,7 +193,8 @@
     barrier = pltpu.get_barrier_semaphore()
 
     def greet(step, carry):
-        peer = (me + 1 + step) % count
+        distance = count // 2 + (1 - 2 * (step % 2)) * ((step + 1) // 2)
+        peer = (me + distance) % count
         pl.semaphore_signal(
             barrier, inc=1, device_id=peer_id(peer, uly_count), device_id_type=MESH
         )
@@ -207,8 +213,22 @@
         loads.append(
             pltpu.make_async_copy(source.at[me], target, in_sem.at[3 + slot])
         )
-    for load in loads:
+    small = []
+    for slot, (source, target) in enumerate(
+        (
+            (vk_gain_hbm, vk_gain),
+            (vq_gain_hbm, vq_gain),
+            (sharp_hbm, sharp),
+            (tk_gain_hbm, tk_gain),
+            (tq_gain_hbm, tq_gain),
+            (valid_hbm, valid),
+        )
+    ):
+        small.append(pltpu.make_async_copy(source, target, in_sem.at[6 + slot]))
+    for load in small + loads:
         load.start()
+    for load in small:
+        load.wait()
 
     sharp_row = sharp[...] / math.sqrt(width)
     square = (heads, heads)
@@ -363,29 +383,32 @@
     def block_rows(index):
         return pl.ds(pl.multiple_of(index * block, block), block)
 
-    text_ones = with_ones(text_kv[...])
-    pairs = plane_pairs(planes[0])
+    def fill(peak, scores):
+        return jnp.concatenate([peak] * (scores.shape[1] // lanes), axis=1)
+
+    def full_peak(scores):
+        return jnp.broadcast_to(row_max(scores), (block, lanes))
+
+    early = group_count // 2
+    pairs = jnp.concatenate([text_kv[...]] + [plane_pairs(plane) for plane in planes[:early]], axis=0)
     ones = with_ones(pairs)
+    wide_bias = jnp.concatenate([bias, jnp.zeros((1, early * block), jnp.float32)], axis=1)
     for index in range(block_count):
-        rows = queries[block_rows(index), :]
-        scores = scores_of(rows, pairs)
-        text_scores = scores_of(rows, text_kv[...]) + bias
-        peak = jnp.maximum(row_max(scores), row_max(text_scores))
-        totals[block_rows(index), :] = weighted(scores, peak, ones) + weighted(
-            text_scores, peak, text_ones
-        )
+        scores = scores_of(queries[block_rows(index), :], pairs) + wide_bias
+        peak = full_peak(scores)
+        totals[block_rows(index), :] = weighted(scores, fill(peak, scores), ones)
         peaks[block_rows(index), :] = peak
 
     def absorb(index, pairs, ones):
         scores = scores_of(queries[block_rows(index), :], pairs)
         earlier = peaks[block_rows(index), :]
-        peak = jnp.maximum(earlier, row_max(scores))
+        peak = jnp.maximum(earlier, full_peak(scores))
         total = totals[block_rows(index), :] * jnp.exp(earlier - peak) + weighted(
-            scores, peak, ones
+            scores, fill(peak, scores), ones
         )
         return peak, total
 
-    for plane in planes[1:-1]:
+    for plane in planes[early:-1]:
         pairs = plane_pairs(plane)
         ones = with_ones(pairs)
         for index in range(block_count):
@@ -406,7 +429,7 @@
     def homeward(peer):
         return pltpu.make_async_remote_copy(
             src_ref=back_send.at[peer],
-            dst_ref=back_recv.at[me],
+            dst_ref=back_out.at[me],
             send_sem=back_send_sem.at[peer],
             recv_sem=back_recv_sem.at[me],
             device_id=peer_id(peer, uly_count),
@@ -416,7 +439,7 @@
     def returned(peer):
         return pltpu.make_async_remote_copy(
             src_ref=back_send.at[peer],
-            dst_ref=back_recv.at[peer],
+            dst_ref=back_out.at[peer],
             send_sem=back_send_sem.at[peer],
             recv_sem=back_recv_sem.at[peer],
             device_id=peer_id(peer, uly_count),
@@ -442,7 +465,8 @@
             return carry
 
         lax.fori_loop(0, group, hand_back, 0)
-    back_recv[me] = back_send[me]
+    own_back = pltpu.make_async_copy(back_send.at[me], back_out.at[me], own_sem.at[0])
+    own_back.start()
 
     attended = jnp.concatenate(
         [attend(index) for index in range(group_count, block_count)], axis=0
@@ -456,7 +480,7 @@
     def text_copy(part, slot):
         return pltpu.make_async_remote_copy(
             src_ref=text_send.at[part],
-            dst_ref=text_recv.at[slot],
+            dst_ref=txt_out.at[slot],
             send_sem=text_send_sem.at[part],
             recv_sem=text_recv_sem.at[slot],
             device_id={"blk": my_blk, "uly": part},
@@ -465,20 +489,20 @@
 
     for step in range(1, uly_count):
         text_copy((my_uly + step) % uly_count, my_uly).start()
-    text_recv[my_uly] = text_send[my_uly]
+    own_text = pltpu.make_async_copy(text_send.at[my_uly], txt_out.at[my_uly], own_sem.at[1])
+    own_text.start()
 
     for step in range(1, uly_count):
         other = (my_uly + step) % uly_count
         text_copy(other, other).wait_recv()
-    txt_out[...] = text_recv[...]
+    own_back.wait()
+    own_text.wait()
 
     def collect(step, carry):
         returned((me + 1 + step) % count).wait_recv()
         return carry
 
     lax.fori_loop(0, count - 1, collect, 0)
-    back_out[...] = back_recv[...]
-
     def drain(step, carry):
         peer = (me + 1 + step) % count
         outward(peer, query_part, q_send_sem, q_recv_sem).wait_send()
@@ -520,8 +544,8 @@
             jax.ShapeDtypeStruct((count, half, lanes), bf16),
             text_shape,
         ),
-        in_specs=[any_spec] * 6 + [vmem_spec] * 6,
-        out_specs=(vmem_spec, vmem_spec),
+        in_specs=[any_spec] * 12,
+        out_specs=(any_spec, any_spec),
         scratch_shapes=[
             pltpu.VMEM((tokens, heads, width), bf16),
             pltpu.VMEM((tokens, heads, width), bf16),
@@ -529,6 +553,12 @@
             pltpu.VMEM((width, text_tokens), bf16),
             pltpu.VMEM((width, text_tokens), bf16),
             pltpu.VMEM((width, text_tokens), bf16),
+            pltpu.VMEM((1, width), f32),
+            pltpu.VMEM((1, width), f32),
+            pltpu.VMEM((1, width), f32),
+            pltpu.VMEM((1, width), f32),
+            pltpu.VMEM((1, heads), f32),
+            pltpu.VMEM((1, text_tokens), jnp.int32),
             pltpu.VMEM((tokens, heads, lanes), f32),
             pltpu.VMEM((half, heads, lanes), f32),
             pltpu.VMEM((count, tokens + half, lanes), bf16),
@@ -536,12 +566,11 @@
             pltpu.VMEM((text_tokens, lanes), bf16),
             pltpu.VMEM((count * tokens + text_tokens, lanes), bf16),
             pltpu.VMEM((count * tokens + text_tokens, lanes), f32),
-            pltpu.VMEM((count * tokens + text_tokens, 1), f32),
-            pltpu.VMEM((count, half, lanes), bf16),
+            pltpu.VMEM((count * tokens + text_tokens, lanes), f32),
             pltpu.VMEM((count, half, lanes), bf16),
             pltpu.VMEM((uly_count, width, text_share), bf16),
-            pltpu.VMEM((uly_count, width, text_share), bf16),
-            dma((6,)),
+            dma((12,)),
+            dma((2,)),
             dma((count,)),
             dma((count,)),
             dma((count,)),
@@ -586,6 +615,7 @@
         and 2 * vq.shape[2] == 128
         and tokens % 32 == 0
         and tokens <= 64
+        and count >= 2 * math.gcd(count, 8)
         and tq.shape[0] % (math.gcd(count, 8) * tokens) == 0
         and tq.shape[0] % (128 * mesh.shape["uly"]) == 0
     )

time: 32.4 us -> 29.6 us (0.914)
  Pallas kernels: 31.6 us -> 28.8 us
    pallas_call x1, Pallas kernels: 29.7 us -> 26.8 us  [fused_on_device(): pl.pallas_call(functools.partial(fused_kernel, blk_count, uly_count), out...]
where the time goes in v4:
time: 29.6 us; the launch traced here: 29.4 us
  Pallas kernels  28.8 us (97%)
  between operations  0.64 us (2%)
    pallas_call x1, Pallas kernels, fused_on_device(): pl.pallas_call(functools.partial(fused_kernel, blk_count, uly_count), out...  26.8 us
    pallas_call x1, Pallas kernels, fused_on_device(): pl.pallas_call(lay_out_kernel, out_shape=(jax.ShapeDtypeStruct((tokens, h...  1.96 us

profile of v4, /device:TPU:0, one launch (start us, length us, event | category | flops | bytes accessed | tf_op | source)
XLA Modules:
  0.0 29.4 jit_solution(265165741265727280)
XLA Ops:
  0.6 26.8 %joint_attention.1 = (bf16[32,16,128]{2,1,0:T(8,128)(2,1)}, bf16[2,64,128]{2,1,0:T(8,128)(2,1)}) custom-call(bf16[32,32,64]{2,1,0:T(8,128)(2,1)} %vq_hbm.1, bf16[32,32,64]{2,1,0:T(8,128)(2,1)} %vk_hbm.1, bf16[32,32,64]{2,1,0:T(8,128)(2,1)} %vv_hbm.1, bf16[32,64,256]{2,1,0:T(8,128)(2,1)} %bitcast.10, bf16[32,64,256]{2,1,0:T(8,128)(2,1)} %bitcast.11, ...), custom_call_target="tpu_custom_call" | custom-call | tf_op jit(solution)/shard_map/joint_attention/pallas_call | solution.py:541
  27.5 2.0 %lay_out.1 = (bf16[32,32,64]{2,1,0:T(8,128)(2,1)}, bf16[2,64,128]{2,1,0:T(8,128)(2,1)}) custom-call(bf16[32,16,128]{2,1,0:T(8,128)(2,1)} %get-tuple-element.6.back_ref, bf16[2,64,128]{2,1,0:T(8,128)(2,1)} %get-tuple-element.7.txt_ref), custom_call_target="tpu_custom_call" | custom-call | tf_op jit(solution)/shard_map/lay_out/pallas_call | solution.py:599

commit v5 on v4

--- a/solution.py
+++ b/solution.py
@@ -580,7 +580,9 @@
             dma((uly_count,)),
             dma((uly_count,)),
         ],
-        compiler_params=pltpu.CompilerParams(collective_id=0, has_side_effects=True),
+        compiler_params=pltpu.CompilerParams(
+            collective_id=0, has_side_effects=True, vmem_limit_bytes=64960 * 1024
+        ),
         name="joint_attention",
     )(
         vq,
@@ -602,6 +604,7 @@
         in_specs=[vmem_spec] * 2,
         out_specs=(vmem_spec, vmem_spec),
         scratch_shapes=[pltpu.VMEM((half, heads, lanes), f32)],
+        compiler_params=pltpu.CompilerParams(vmem_limit_bytes=8 * 1024 * 1024),
         name="lay_out",
     )(back, text_back)
     return vid_out, jnp.transpose(txt_out, (2, 0, 1))

time: 29.6 us -> 30.4 us (1.027)
  local copies, waits for them, and re-layouts: 0 us -> 1.65 us
  Pallas kernels: 28.8 us -> 27.9 us
    unnamed x0 -> x4, local copies, waits for them, and re-layouts: none -> 1.65 us
    pallas_call x1, Pallas kernels: 1.96 us -> 1.05 us  [fused_on_device(): pl.pallas_call(lay_out_kernel, out_shape=(jax.ShapeDtypeStruct((tokens, h...]
where the time goes in v5:
time: 30.4 us; the launch traced here: 30.2 us
  Pallas kernels  27.9 us (92%)
  local copies, waits for them, and re-layouts  1.65 us (5%)
  between operations  0.65 us (2%)
    pallas_call x1, Pallas kernels, fused_on_device(): pl.pallas_call(functools.partial(fused_kernel, blk_count, uly_count), out...  26.8 us
    unnamed x4, local copies, waits for them, and re-layouts  1.65 us
    pallas_call x1, Pallas kernels, fused_on_device(): pl.pallas_call(lay_out_kernel, out_shape=(jax.ShapeDtypeStruct((tokens, h...  1.05 us

profile of v5, /device:TPU:0, one launch (start us, length us, event | category | flops | bytes accessed | tf_op | source)
XLA Modules:
  0.0 30.2 jit_solution(18437106282082559185)
XLA Ops:
  0.6 26.8 %joint_attention.1 = (bf16[32,16,128]{2,1,0:T(8,128)(2,1)}, bf16[2,64,128]{2,1,0:T(8,128)(2,1)}) custom-call(bf16[32,32,64]{2,1,0:T(8,128)(2,1)} %vq_hbm.1, bf16[32,32,64]{2,1,0:T(8,128)(2,1)} %vk_hbm.1, bf16[32,32,64]{2,1,0:T(8,128)(2,1)} %vv_hbm.1, bf16[32,64,256]{2,1,0:T(8,128)(2,1)} %bitcast.10, bf16[32,64,256]{2,1,0:T(8,128)(2,1)} %bitcast.11, ...), custom_call_target="tpu_custom_call" | custom-call | tf_op jit(solution)/shard_map/joint_attention/pallas_call | solution.py:541
  27.5 0.0 copy-start
  27.5 0.9 %copy-done = bf16[32,16,128]{2,1,0:T(8,128)(2,1)S(1)} copy-done((bf16[32,16,128]{2,1,0:T(8,128)(2,1)S(1)}, bf16[32,16,128]{2,1,0:T(8,128)(2,1)}, u32[]{:S(2)}) %copy-start) | copy-done | bytes 131096
  28.4 0.0 copy-start.1
  28.4 0.8 %copy-done.1 = bf16[2,64,128]{2,1,0:T(8,128)(2,1)S(1)} copy-done((bf16[2,64,128]{2,1,0:T(8,128)(2,1)S(1)}, bf16[2,64,128]{2,1,0:T(8,128)(2,1)}, u32[]{:S(2)}) %copy-start.1) | copy-done | bytes 32792
  29.1 1.1 %lay_out.1 = (bf16[32,32,64]{2,1,0:T(8,128)(2,1)}, bf16[2,64,128]{2,1,0:T(8,128)(2,1)}) custom-call(bf16[32,16,128]{2,1,0:T(8,128)(2,1)S(1)} %copy-done, bf16[2,64,128]{2,1,0:T(8,128)(2,1)S(1)} %copy-done.1), custom_call_target="tpu_custom_call" | custom-call | tf_op jit(solution)/shard_map/lay_out/pallas_call | solution.py:601
Async XLA Ops:
  27.5 0.9 %copy-start = (bf16[32,16,128]{2,1,0:T(8,128)(2,1)S(1)}, bf16[32,16,128]{2,1,0:T(8,128)(2,1)}, u32[]{:S(2)}) copy-start(bf16[32,16,128]{2,1,0:T(8,128)(2,1)} %get-tuple-element.6.back_ref) | copy-start | bytes 393220
  28.4 0.8 %copy-start.1 = (bf16[2,64,128]{2,1,0:T(8,128)(2,1)S(1)}, bf16[2,64,128]{2,1,0:T(8,128)(2,1)}, u32[]{:S(2)}) copy-start(bf16[2,64,128]{2,1,0:T(8,128)(2,1)} %get-tuple-element.7.txt_ref) | copy-start | bytes 98308
